TPU v7x, 512 devices: a whole 4x4x16 slice. The times are simulated.
512 devices in a mesh: dp: 128 (over x, z, core), mp: 4 (over y).
Axes of the slice: x: 4, y: 4, z: 16, core: 2. Of those that a mesh axis runs over, the one named last changes fastest.
Arguments:
- gating_logits: bfloat16 [128, 3, 64, 7168], P('dp', None, None, 'mp'), may hold values from -6 to 6
- lifted_hidden_values: bfloat16 [128, 3, 64, 7168], P('dp', None, None, 'mp'), may hold values from -6 to 6
- loss_output_grad: bfloat16 [128, 3, 64, 2048], P('dp', None, None, 'mp'), may hold values from -1792 to 1792
- arrival_flags: int32 [128], P('dp'), may hold values from 0 to 1, as said below
- block_owner_map: int32 [128, 3], P('dp'), may hold values from 0 to 127, as said below
- decoder_multipliers: int32 [128, 3], P('dp'), may hold values from 1 to 4
- block_piece_number: int32 [128], replicated, may hold values from 1 to 2, as said below
Outputs:
- down_grad: float32 [2048, 7168], P('dp', 'mp')
Inputs may be any that keep to these rules, and one draw needn't show every extreme that they name: `arrival_flags`: at least one replica survives. `block_owner_map`: row i lists the partitions (i + r + k) mod 128 for k < 3, with one r for all rows. `block_piece_number`: some partition has exactly 2 live tiles.
All inputs are finite; a program needn't handle non-finite values.
Results may differ from a plain program's by a relative error of at most 0.0042.
Values may be sent and summed in bfloat16 or wider, within the bound.
A program may use at most 128 MiB of HBM per device.

v0:
```python
import jax
import jax.numpy as jnp
from jax import lax
from jax.sharding import PartitionSpec as P

TILE = 32


def copy_for_each(shard, axis):
    count = lax.axis_size(axis)
    return lax.all_to_all(
        jnp.broadcast_to(shard[None], (count, *shard.shape)), axis, 0, 0, tiled=True
    )


def laid_out(pieces, dim):
    shape = list(pieces.shape[1:])
    shape[dim] *= pieces.shape[0]
    return jnp.moveaxis(pieces, 0, dim).reshape(shape)


def collect(shard, axis, dim):
    pieces = copy_for_each(shard, axis)
    return laid_out(pieces, dim)


def slot_product(columns, hidden_k):
    return lax.dot_general(
        columns, hidden_k, (((0,), (0,)), ((), ())), preferred_element_type=jnp.float32
    )


def on_device(
    gating_logits,
    lifted_hidden_values,
    loss_output_grad,
    arrival_flags,
    block_owner_map,
    decoder_multipliers,
    block_piece_number,
):
    slot_tally = gating_logits.shape[1]
    tok_rows = gating_logits.shape[2]
    part_ids = jnp.arange(block_piece_number.shape[0], dtype=jnp.int32)
    slot_tiles = jnp.sum(
        jnp.where(block_owner_map[0][:, None] == part_ids[None, :], block_piece_number[None, :], 0),
        axis=1,
    )
    live_rows = slot_tiles * TILE
    live_mask = jnp.arange(tok_rows, dtype=jnp.int32)[None, :] < live_rows[:, None]
    hidden = (
        jax.nn.silu(gating_logits[0].astype(jnp.float32))
        * lifted_hidden_values[0].astype(jnp.float32)
        * live_mask[:, :, None].astype(jnp.float32)
    ).astype(jnp.bfloat16)
    down_kernel_array = arrival_flags[0].astype(jnp.float32) * decoder_multipliers[0].astype(
        jnp.float32
    )
    token_sum = jnp.sum(down_kernel_array * live_rows.astype(jnp.float32))
    cotangent = collect(loss_output_grad, "mp", 3)[0]
    feature_total = cotangent.shape[2]
    block_count = 8
    block_rows = feature_total // block_count

    def project(carry, block_num):
        columns = lax.dynamic_slice_in_dim(cotangent, block_num * block_rows, block_rows, 2)
        running_total = jnp.zeros((block_rows, hidden.shape[2]), jnp.float32)
        for slot_num in range(slot_tally):
            product = slot_product(columns[slot_num], hidden[slot_num])
            running_total = running_total + down_kernel_array[slot_num] * product
        return (carry, running_total)

    _, blocks = lax.scan(
        project, jnp.zeros((), jnp.float32), jnp.arange(block_count, dtype=jnp.int32)
    )
    gradient = blocks.reshape(feature_total, hidden.shape[2])
    replicas = lax.axis_size("dp")
    stacked = gradient.reshape(replicas, feature_total // replicas, hidden.shape[2])
    count_col = jnp.full((replicas, 1), token_sum, jnp.float32)
    received, counts_in = (
        lax.all_to_all(
            stacked.astype(jnp.bfloat16), "dp", split_axis=0, concat_axis=0, tiled=True
        ).astype(stacked.dtype),
        lax.all_to_all(
            count_col.astype(jnp.bfloat16), "dp", split_axis=0, concat_axis=0, tiled=True
        ).astype(count_col.dtype),
    )
    total_tokens = jnp.sum(counts_in)
    return jnp.sum(received, axis=0) / total_tokens


def solution(mesh):
    return jax.shard_map(
        on_device,
        mesh=mesh,
        in_specs=(
            P("dp", None, None, "mp"),
            P("dp", None, None, "mp"),
            P("dp", None, None, "mp"),
            P("dp"),
            P("dp", None),
            P("dp", None),
            P(),
        ),
        out_specs=P("dp", "mp"),
        check_vma=False,
    )
```

profile of v0, /device:TPU:1, one launch (start us, length us, event | category | flops | bytes accessed | tf_op | source)
XLA Modules:
  0.0 453.6 jit_solution(7620118042625257169)
XLA Ops:
  0.0 0.0 copy-start
  0.0 0.0 copy-start.1
  0.0 2.0 broadcast_in_dim.37
  2.0 5.0 %all-to-all-start = ((bf16[4,1,3,64,512]{4,3,2,1,0:T(8,128)(2,1)}), bf16[4,1,3,64,512]{4,3,2,1,0:T(8,128)(2,1)S(1)}, u32[]{:S(2)}, u32[]{:S(2)}) async-start(bf16[4,1,3,64,512]{4,3,2,1,0:T(8,128)(2,1)} %broadcast_in_dim.37), calls=%async_computation | async-start | bytes 1572864 | tf_op jit(solution)/shard_map/all_to_all | solution.py:11
  7.7 0.0 copy-done.4
  7.7 0.0 copy-done.3
  7.7 0.2 select_reduce_fusion
  7.9 0.1 fusion.19
  8.0 0.0 copy-done.2
  8.0 0.6 multiply_reduce_fusion
  8.6 0.5 fusion.18
  9.1 6.3 %all-to-all-done = bf16[4,1,3,64,512]{4,3,2,1,0:T(8,128)(2,1)S(1)} async-done(((bf16[4,1,3,64,512]{4,3,2,1,0:T(8,128)(2,1)}), bf16[4,1,3,64,512]{4,3,2,1,0:T(8,128)(2,1)S(1)}, u32[]{:S(2)}, u32[]{:S(2)}) %all-to-all-start) | async-done | bytes 786464 | tf_op jit(solution)/shard_map/all_to_all | solution.py:11
  15.4 1.2 broadcast_in_dim.40
  16.6 23.8 %all-to-all-start.2 = ((bf16[128,1,1]{2,1,0:T(2,128)(2,1)}), bf16[128,1,1]{2,1,0:T(2,128)(2,1)S(1)}, u32[]{:S(2)}, u32[]{:S(2)}) async-start(bf16[128,1,1]{2,1,0:T(2,128)(2,1)} %broadcast_in_dim.40), calls=%async_computation.2 | async-start | bytes 131072 | tf_op jit(solution)/shard_map/all_to_all | solution.py:84
  40.4 0.6 copy.12
  41.0 0.6 squeeze_reshape.3
  41.6 71.4 %while.10 = (s32[]{:T(128)}, bf16[8,256,1792]{2,1,0:T(8,128)(2,1)}, f32[3]{0:T(128)S(1)}, s32[8]{0:T(128)S(1)}, bf16[3,64,2048]{2,1,0:T(8,128)(2,1)S(1)}, /*inde...) while((s32[]{:T(128)}, bf16[8,256,1792]{2,1,0:T(8,128)(2,1)}, ...), condition=%wide.region_2.3_spmd, body=%wide.region_1.2_spmd.sunk | while | flops 178454528 | bytes 9962747 | solution.py:73
  41.6 0.7 dynamic_slice.8
  42.9 0.7 fusion.30
  43.6 2.4 convolution_multiply_fusion.4
  46.0 2.6 fusion.31
  48.6 1.9 fusion.32
  50.5 0.6 dynamic_slice.8
  51.9 0.7 fusion.30
  52.5 2.4 convolution_multiply_fusion.4
  54.9 2.6 fusion.31
  57.5 2.0 fusion.32
  59.5 0.6 dynamic_slice.8
  60.8 0.7 fusion.30
  61.5 2.4 convolution_multiply_fusion.4
  63.9 2.6 fusion.31
  66.4 1.9 fusion.32
  68.4 0.6 dynamic_slice.8
  69.7 0.7 fusion.30
  70.4 2.4 convolution_multiply_fusion.4
  72.8 2.6 fusion.31
  75.3 2.0 fusion.32
  77.3 0.6 dynamic_slice.8
  78.6 0.7 fusion.30
  79.3 2.4 convolution_multiply_fusion.4
  81.7 2.6 fusion.31
  84.3 1.9 fusion.32
  86.2 0.6 dynamic_slice.8
  87.5 0.7 fusion.30
  88.2 2.4 convolution_multiply_fusion.4
  90.6 2.5 fusion.31
  93.2 1.9 fusion.32
  95.1 0.6 dynamic_slice.8
  96.5 0.7 fusion.30
  97.1 2.4 convolution_multiply_fusion.4
  99.6 2.6 fusion.31
  102.1 2.0 fusion.32
  104.1 0.6 dynamic_slice.8
  105.4 0.7 fusion.30
  106.1 2.4 convolution_multiply_fusion.4
  108.5 2.6 fusion.31
  111.1 2.0 fusion.32
  113.0 0.0 all-to-all-done.2
  113.0 16.6 %all-to-all-start.1 = ((bf16[128,16,1792]{2,1,0:T(8,128)(2,1)}), bf16[128,16,1792]{2,1,0:T(8,128)(2,1)}, u32[]{:S(2)}, u32[]{:S(2)}) async-start(bf16[128,16,1792]{2,1,0:T(8,128)(2,1)} %bitcast.62), calls=%async_computation.1 | async-start | bytes 14680064 | tf_op jit(solution)/shard_map/all_to_all | solution.py:81
  129.6 0.1 copy.13
  129.7 0.7 convert_reduce_fusion.1
  130.4 317.7 %all-to-all-done.1 = bf16[128,16,1792]{2,1,0:T(8,128)(2,1)} async-done(((bf16[128,16,1792]{2,1,0:T(8,128)(2,1)}), bf16[128,16,1792]{2,1,0:T(8,128)(2,1)}, u32[]{:S(2)}, u32[]{:S(2)}) %all-to-all-start.1) | async-done | bytes 7340064 | tf_op jit(solution)/shard_map/all_to_all | solution.py:81
  448.1 4.1 convert_reduce_fusion
  452.2 1.3 broadcast_divide_fusion
  (8 shorter events, 0.0 us)
Async XLA Ops:
  0.0 7.7 %copy-start.4 = (s32[1,3]{1,0:T(1,128)S(1)}, s32[1,3]{1,0:T(1,128)}, u32[]{:S(2)}) copy-start(s32[1,3]{1,0:T(1,128)} %param.13) | copy-start | bytes 40
  0.0 7.7 %copy-start.3 = (s32[128]{0:T(128)S(1)}, s32[128]{0:T(128)}, u32[]{:S(2)}) copy-start(s32[128]{0:T(128)} %param.15) | copy-start | bytes 1540
  0.0 8.0 %copy-start.2 = (s32[1,3]{1,0:T(1,128)S(1)}, s32[1,3]{1,0:T(1,128)}, u32[]{:S(2)}) copy-start(s32[1,3]{1,0:T(1,128)} %param.14) | copy-start | bytes 40
  0.0 8.6 %copy-start = (bf16[1,3,64,1792]{3,2,1,0:T(8,128)(2,1)S(1)}, bf16[1,3,64,1792]{3,2,1,0:T(8,128)(2,1)}, u32[]{:S(2)}) copy-start(bf16[1,3,64,1792]{3,2,1,0:T(8,128)(2,1)} %param.10) | copy-start | bytes 2064388
  0.0 8.5 %copy-start.1 = (bf16[1,3,64,1792]{3,2,1,0:T(8,128)(2,1)S(1)}, bf16[1,3,64,1792]{3,2,1,0:T(8,128)(2,1)}, u32[]{:S(2)}) copy-start(bf16[1,3,64,1792]{3,2,1,0:T(8,128)(2,1)} %param.9) | copy-start | bytes 2064388
  2.0 13.3 %all-to-all-start = ((bf16[4,1,3,64,512]{4,3,2,1,0:T(8,128)(2,1)}), bf16[4,1,3,64,512]{4,3,2,1,0:T(8,128)(2,1)S(1)}, u32[]{:S(2)}, u32[]{:S(2)}) async-start(bf16[4,1,3,64,512]{4,3,2,1,0:T(8,128)(2,1)} %broadcast_in_dim.37), calls=%async_computation | async-start | bytes 1572864 | tf_op jit(solution)/shard_map/all_to_all | solution.py:11
  16.6 96.4 %all-to-all-start.2 = ((bf16[128,1,1]{2,1,0:T(2,128)(2,1)}), bf16[128,1,1]{2,1,0:T(2,128)(2,1)S(1)}, u32[]{:S(2)}, u32[]{:S(2)}) async-start(bf16[128,1,1]{2,1,0:T(2,128)(2,1)} %broadcast_in_dim.40), calls=%async_computation.2 | async-start | bytes 131072 | tf_op jit(solution)/shard_map/all_to_all | solution.py:84
  113.0 335.1 %all-to-all-start.1 = ((bf16[128,16,1792]{2,1,0:T(8,128)(2,1)}), bf16[128,16,1792]{2,1,0:T(8,128)(2,1)}, u32[]{:S(2)}, u32[]{:S(2)}) async-start(bf16[128,16,1792]{2,1,0:T(8,128)(2,1)} %bitcast.62), calls=%async_computation.1 | async-start | bytes 14680064 | tf_op jit(solution)/shard_map/all_to_all | solution.py:81
where the time goes:
time: 458 us; the launch traced here: 454 us
  waiting for transfers between devices  324 us (71%)
  matrix products  55.4 us (12%)
  starting transfers between devices  45.4 us (10%)
  local copies, waits for them, and re-layouts  15 us (3%)
  other arithmetic  7.54 us (2%)
  loops' own time  5.55 us (1%)
    all_to_all x1, waiting for transfers between devices, on_device(): lax.all_to_all(stacked.astype(jnp.bfloat16), 'dp', split_axis=0, concat_a...  318 us
    dot_general x24, matrix products, slot_product(): lax.dot_general(columns, hidden_k, (((0,), (0,)), ((), ())), preferred_el...  55.4 us
    all_to_all x1, starting transfers between devices, on_device(): lax.all_to_all(count_col.astype(jnp.bfloat16), 'dp', split_axis=0, concat...  23.8 us
    all_to_all x1, starting transfers between devices, on_device(): lax.all_to_all(stacked.astype(jnp.bfloat16), 'dp', split_axis=0, concat_a...  16.6 us
  transfers between devices with their start and end apart: 3, of which 2 were waited for; matrix products, arithmetic and copies ran while one was open for 15% of the time, Pallas kernels for 0%

commit v1 on v0

v1 whole, which is shorter than its diff:
```python
import functools

import jax
import jax.numpy as jnp
from jax import lax
from jax.experimental import pallas as pl
from jax.experimental.pallas import tpu as pltpu
from jax.sharding import PartitionSpec as P

MESH = pl.DeviceIdType.MESH
TILE = 32
NX = 4
NY = 4
NC = 2
PAD = 16
WIDTHS = (384, 256, 256)
STAGGER = 3
CHAINS = ((1, (7, 6, 5, 4, 3, 2, 1, 0)), (-1, (8, 7, 6, 5, 4, 3, 2, 1, 0)))
SEMS = 192


def kernel(
    nz, slots, tok,
    gate_hbm, lift_hbm, cot_hbm, arrival, owner, mult, pieces,
    out,
    gate, lift, cot, in_sem,
    Y, TU, TD, C, CT, H, HS, PR, ZS, ZR, CS, CR, R, FR, cnt_z,
    ssem, rsem,
):
    T = slots * tok
    TP = T + PAD
    nq = len(WIDTHS)
    half = sum(WIDTHS)
    offs = [sum(WIDTHS[:q]) for q in range(nq)]
    LO = (T // 2) // 16 * 16

    dp = lax.axis_index("dp")
    y = lax.axis_index("mp")
    x = dp // (NC * nz)
    z = (dp // NC) % nz
    c = dp % NC

    def dev(dx=0, dy=0, dz=0, flip=False):
        xx = (x + dx + NX) % NX
        yy = (y + dy + NY) % NY
        zz = (z + dz + nz) % nz
        cc = 1 - c if flip else c
        return (xx * (NC * nz) + zz * NC + cc, yy)

    ids = iter(range(SEMS))
    every = []

    def send(src, dst, to):
        i = next(ids)
        d = pltpu.make_async_remote_copy(
            src_ref=src, dst_ref=dst, send_sem=ssem.at[i], recv_sem=rsem.at[i],
            device_id=to, device_id_type=MESH,
        )
        d.start()
        every.append(d)
        return d

    loads = [
        pltpu.make_async_copy(cot_hbm, cot, in_sem.at[0]),
        pltpu.make_async_copy(gate_hbm, gate, in_sem.at[1]),
        pltpu.make_async_copy(lift_hbm, lift, in_sem.at[2]),
    ]
    for d in loads:
        d.start()

    hops = sorted({a - b for _, dist in CHAINS for a, b in zip(dist, dist[1:])})
    near = [dev(flip=True), dev(dx=1), dev(dx=-1), dev(dy=1), dev(dy=-1)]
    for h in hops:
        near += [dev(dz=h), dev(dz=-h)]
    barrier = pltpu.get_barrier_semaphore()
    for n in near:
        pl.semaphore_signal(barrier, inc=1, device_id=n, device_id_type=MESH)
    pl.semaphore_wait(barrier, len(near))

    tiles = [pieces[owner[0, k]] for k in range(slots)]
    weights = [arrival[0] * mult[0, k] for k in range(slots)]
    count = sum(w * t for w, t in zip(weights, tiles)).astype(jnp.float32)

    loads[0].wait()
    for k in range(slots):
        rows = pl.ds(k * tok, tok)
        Y[0, rows, :] = (cot[rows, :].astype(jnp.float32) * weights[k].astype(jnp.float32)).astype(jnp.bfloat16)
    Y[0, pl.ds(T, PAD), :] = jnp.full((PAD, Y.shape[2]), count, jnp.float32).astype(jnp.bfloat16)
    y_up = send(Y.at[0], Y.at[3], dev(dy=1))
    y_dn = send(Y.at[0], Y.at[1], dev(dy=-1))

    for q in range(nq):
        for r in range(NX):
            for k in range(NC):
                H[q][r, k, pl.ds(T, PAD), :] = jnp.zeros((PAD, WIDTHS[q]), jnp.bfloat16)

    loads[1].wait()
    loads[2].wait()

    def hidden(k, which, q):
        rows = pl.ds(k * tok, tok)
        cols = pl.ds(pl.multiple_of(which * half + offs[q], 128), WIDTHS[q])
        g = gate[rows, cols].astype(jnp.float32)
        u = lift[rows, cols].astype(jnp.float32)
        h = g / (1.0 + jnp.exp(-g)) * u
        row = lax.broadcasted_iota(jnp.int32, h.shape, 0)
        return jnp.where(row < tiles[k] * TILE, h, 0.0).astype(jnp.bfloat16)

    body = pl.ds(0, T)
    h_core, h_up, h_dn = {}, {}, {}

    def x_send(q, k):
        h_up[q, k] = send(H[q].at[0, k, body], H[q].at[3, k, body], dev(dx=1))
        h_dn[q, k] = send(H[q].at[0, k, body], H[q].at[1, k, body], dev(dx=-1))

    for q in range(nq):
        for k in range(slots):
            HS[q][pl.ds(k * tok, tok), :] = hidden(k, 1 - c, q)
        h_core[q] = send(HS[q], H[q].at[0, 1, body], dev(flip=True))
        for k in range(slots):
            H[q][0, 0, pl.ds(k * tok, tok), :] = hidden(k, c, q)
        if q < 2:
            x_send(q, 0)
        if q == 0:
            h_core[0].wait_recv()
            x_send(0, 1)

    y_up.wait_recv()
    y_fup = send(Y.at[3, pl.ds(LO, TP - LO)], Y.at[2, pl.ds(LO, TP - LO)], dev(dy=1))
    y_dn.wait_recv()
    y_fdn = send(Y.at[1, pl.ds(0, LO)], Y.at[2, pl.ds(0, LO)], dev(dy=-1))
    y_fup.wait_recv()
    y_fdn.wait_recv()

    far = (x + 2 + NY - y) % NY
    c_tu = send(Y.at[far, pl.ds(0, LO)], TU, dev(dx=1))
    c_td = send(Y.at[far, pl.ds(LO, TP - LO)], TD, dev(dx=-1))
    c_up = send(Y.at[(x + 1 + NY - y) % NY], C.at[3, 0], dev(dx=1))
    c_dn = send(Y.at[(x - 1 + NX + NY - y) % NY], C.at[1, 0], dev(dx=-1))
    mine = (x + NY - y) % NY
    c_core = {0: send(Y.at[mine], C.at[0, 1], dev(flip=True))}
    C[0, 0] = Y[mine]

    h_f = {}

    def forward(q):
        h_dn[q, 0].wait_recv()
        h_f[q, 0] = send(H[q].at[1, 0, body], H[q].at[2, 0, body], dev(dx=-1))
        h_up[q, 1].wait_recv()
        h_f[q, 1] = send(H[q].at[3, 1, body], H[q].at[2, 1, body], dev(dx=1))

    h_core[1].wait_recv()
    x_send(1, 1)
    c_tu.wait_recv()
    c_fu = send(TU, C.at[2, 0, pl.ds(0, LO)], dev(dx=1))
    c_td.wait_recv()
    c_fd = send(TD, C.at[2, 0, pl.ds(LO, TP - LO)], dev(dx=-1))
    forward(0)
    for q in range(2, nq):
        x_send(q, 0)
        h_core[q].wait_recv()
        x_send(q, 1)
    c_up.wait_recv()
    c_core[3] = send(C.at[3, 0], C.at[3, 1], dev(flip=True))
    c_dn.wait_recv()
    c_core[1] = send(C.at[1, 0], C.at[1, 1], dev(flip=True))
    forward(1)
    c_fu.wait_recv()
    c_fd.wait_recv()
    c_core[2] = send(C.at[2, 0], C.at[2, 1], dev(flip=True))
    for q in range(2, nq):
        forward(q)
    for r in range(NX):
        c_core[r].wait_recv()

    whole = C[...].reshape(NX * NC * TP, C.shape[3])
    CT[...] = whole.T
    cz = jnp.zeros((PAD, 128), jnp.float32)
    for r in range(NX):
        for k in range(NC):
            cz = cz + C[r, k, pl.ds(T, PAD), pl.ds(0, 128)].astype(jnp.float32)
    cnt_z[...] = cz

    base = []
    n = 0
    for _, dist in CHAINS:
        base.append(n)
        n += len(dist) - 1
    msgs = {}

    def z_step(q, s):
        for ci, (sign, dist) in enumerate(CHAINS):
            if s >= len(dist) - 1:
                continue
            slot = base[ci] + s
            own = (z + sign * dist[s] + nz) % nz
            to = dev(dz=sign * (dist[s] - dist[s + 1]))
            v = PR[q][own]
            if s > 0:
                msgs[q, ci, s - 1].wait_recv()
                v = v + ZR[q][slot - 1].astype(jnp.float32)
            ZS[q][slot] = v.astype(jnp.bfloat16)
            msgs[q, ci, s] = send(ZS[q].at[slot], ZR[q].at[slot], to)
            if q == 0:
                w = cnt_z[...]
                if s > 0:
                    msgs["c", ci, s - 1].wait_recv()
                    w = w + CR[slot - 1]
                CS[slot] = w
                msgs["c", ci, s] = send(CS.at[slot], CR.at[slot], to)

    steps = max(len(d) for _, d in CHAINS) - 1
    for t in range((nq - 1) * STAGGER + steps):
        for q in range(nq):
            s = t - q * STAGGER
            if s == 0:
                for d in (h_up[q, 0], h_dn[q, 1], h_f[q, 0], h_f[q, 1]):
                    d.wait_recv()
                rhs = H[q][...].reshape(NX * NC * TP, WIDTHS[q])
                for m in range(4):
                    acc = jnp.dot(CT[pl.ds(m * 128, 128), :], rhs, preferred_element_type=jnp.float32)
                    PR[q][pl.ds(m * (nz // 4), nz // 4)] = acc.reshape(nz // 4, 128 * 4 // nz, WIDTHS[q])
            if 0 <= s < steps:
                z_step(q, s)

    fin = {}
    total = cnt_z[...]
    for ci, (_, dist) in enumerate(CHAINS):
        msgs["c", ci, len(dist) - 2].wait_recv()
        total = total + CR[base[ci] + len(dist) - 2]
    total = total[0:1, 0:1] * float(TILE)
    for q in range(nq):
        v = PR[q][z]
        for ci, (_, dist) in enumerate(CHAINS):
            msgs[q, ci, len(dist) - 2].wait_recv()
            v = v + ZR[q][base[ci] + len(dist) - 2].astype(jnp.float32)
        R[q][...] = (v / total).reshape(R[q].shape)
        fin[q] = send(R[q].at[1 - c], FR[q], dev(flip=True))
        out[:, pl.ds(pl.multiple_of(c * half + offs[q], 128), WIDTHS[q])] = R[q][c]
    for q in range(nq):
        fin[q].wait_recv()
        out[:, pl.ds(pl.multiple_of((1 - c) * half + offs[q], 128), WIDTHS[q])] = FR[q][...]
    for d in every:
        d.wait_send()


def on_device(nz, gate, lift, cot, arrival, owner, mult, pieces):
    _, slots, tok, ff = gate.shape
    db = cot.shape[3]
    T, TP = slots * tok, slots * tok + PAD
    LO = (T // 2) // 16 * 16
    rows = db // nz
    n = sum(len(d) - 1 for _, d in CHAINS)
    bf, f32 = jnp.bfloat16, jnp.float32
    V = pltpu.VMEM
    any_ = pl.BlockSpec(memory_space=pl.ANY)
    smem = pl.BlockSpec(memory_space=pltpu.SMEM)
    return pl.pallas_call(
        functools.partial(kernel, nz, slots, tok),
        out_shape=jax.ShapeDtypeStruct((rows // NC, ff), f32),
        in_specs=[any_, any_, any_, smem, smem, smem, smem],
        out_specs=pl.BlockSpec(memory_space=pltpu.VMEM),
        scratch_shapes=[
            V((T, ff), bf), V((T, ff), bf), V((T, db), bf), pltpu.SemaphoreType.DMA((3,)),
            V((NY, TP, db), bf), V((LO, db), bf), V((TP - LO, db), bf),
            V((NX, NC, TP, db), bf), V((db, NX * NC * TP), bf),
            [V((NX, NC, TP, w), bf) for w in WIDTHS],
            [V((T, w), bf) for w in WIDTHS],
            [V((nz, rows, w), f32) for w in WIDTHS],
            [V((n, rows, w), bf) for w in WIDTHS],
            [V((n, rows, w), bf) for w in WIDTHS],
            V((n, PAD, 128), f32), V((n, PAD, 128), f32),
            [V((NC, rows // NC, w), f32) for w in WIDTHS],
            [V((rows // NC, w), f32) for w in WIDTHS],
            V((PAD, 128), f32),
            pltpu.SemaphoreType.DMA((SEMS,)), pltpu.SemaphoreType.DMA((SEMS,)),
        ],
        compiler_params=pltpu.CompilerParams(
            collective_id=0, has_side_effects=True, vmem_limit_bytes=60 * 1024 * 1024
        ),
    )(
        gate.reshape(T, ff), lift.reshape(T, ff), cot.reshape(T, db),
        arrival, owner, mult, pieces,
    )


def solution(mesh):
    nz = mesh.shape["dp"] // (NX * NC)
    return jax.shard_map(
        functools.partial(on_device, nz),
        mesh=mesh,
        in_specs=(
            P("dp", None, None, "mp"),
            P("dp", None, None, "mp"),
            P("dp", None, None, "mp"),
            P("dp"),
            P("dp", None),
            P("dp", None),
            P(),
        ),
        out_specs=P("dp", "mp"),
        check_vma=False,
    )
```

time: 458 us -> 99.2 us (0.22)
  waiting for transfers between devices: 324 us -> 0 us
  Pallas kernels: 0 us -> 96.8 us
  matrix products: 55.4 us -> 0 us
  starting transfers between devices: 45.4 us -> 0 us
  local copies, waits for them, and re-layouts: 15 us -> 1.55 us
  other arithmetic: 7.54 us -> 0 us
  loops' own time: 5.55 us -> 0 us
    all_to_all x3 -> x0, waiting for transfers between devices: 324 us -> none  [the longest x1 318 us: on_device(): lax.all_to_all(stacked.astype(jnp.bfloat16), 'dp', split_axis=0, concat_a...]
    pallas_call x0 -> x1, Pallas kernels: none -> 96.8 us  [on_device(): pl.pallas_call(functools.partial(kernel, nz, slots, tok), out_shape=jax.S...]
    dot_general x24 -> x0, matrix products: 55.4 us -> none  [slot_product(): lax.dot_general(columns, hidden_k, (((0,), (0,)), ((), ())), preferred_el...]
    all_to_all x3 -> x0, starting transfers between devices: 45.4 us -> none  [the longest x1 23.8 us: on_device(): lax.all_to_all(count_col.astype(jnp.bfloat16), 'dp', split_axis=0, concat...]
    reduce_sum x4 -> x0, other arithmetic: 5.6 us -> none  [the longest x1 4.12 us: on_device(): return jnp.sum(received, axis=0) / total_tokens]
    another operation x1 -> x0, loops' own time: 5.55 us -> none  [on_device(): lax.scan(project, jnp.zeros((), jnp.float32), jnp.arange(block_count, dty...]
    slice x8 -> x0, local copies, waits for them, and re-layouts: 5.31 us -> none  [project(): running_total = running_total + down_kernel_array[slot_num] * product]
    dynamic_slice x8 -> x0, local copies, waits for them, and re-layouts: 5.17 us -> none  [on_device(): lax.scan(project, jnp.zeros((), jnp.float32), jnp.arange(block_count, dty...]
  transfers between devices with their start and end apart: 3 -> 0, of which waited for: 2 -> 0; matrix products, arithmetic and copies ran while one was open for 15% -> 0% of each run, Pallas kernels for 0% -> 0%
where the time goes in v1:
time: 99.2 us; the launch traced here: 99 us
  Pallas kernels  96.8 us (98%)
  local copies, waits for them, and re-layouts  1.55 us (2%)
    pallas_call x1, Pallas kernels, on_device(): pl.pallas_call(functools.partial(kernel, nz, slots, tok), out_shape=jax.S...  96.8 us

profile of v1, /device:TPU:1, one launch (start us, length us, event | category | flops | bytes accessed | tf_op | source)
XLA Modules:
  0.0 99.0 jit_solution(7025079193974132556)
XLA Ops:
  0.7 96.8 %shard_map.73 = f32[16,1792]{1,0:T(8,128)} custom-call(bf16[192,1792]{1,0:T(8,128)(2,1)} %bitcast.3, bf16[192,1792]{1,0:T(8,128)(2,1)} %bitcast.4, bf16[192,512]{1,0:T(8,128)(2,1)} %bitcast.5, s32[1]{0:T(128)S(6)} %copy.9.arrival, s32[1,3]{1,0:T(1,128)} %owner.1, s32[1,3]{1,0:T(1,128)} %mult.1, s32[128]{0:T(128)} %pieces.1), custom_call_target="tpu_custom_call" | custom-call | tf_op jit(solution)/shard_map/pallas_call | solution.py:258
  97.5 1.6 %copy.10 = f32[16,1792]{1,0:T(8,128)} copy(f32[16,1792]{1,0:T(8,128)} %shard_map.73) | data formatting | bytes 229376

commit v2 on v1

v2 whole, which is shorter than its diff:
```python
import functools

import jax
import jax.numpy as jnp
from jax import lax
from jax.experimental import pallas as pl
from jax.experimental.pallas import tpu as pltpu
from jax.sharding import PartitionSpec as P

MESH = pl.DeviceIdType.MESH
TILE = 32
NX = 4
NY = 4
NC = 2
WIDTHS = (256, 256, 256, 128)
SKIP2 = ((-1, (8, 6, 4, 2, 0)), (1, (7, 5, 3, 1, 0)), (-1, (7, 5, 3, 1, 0)), (1, (6, 4, 2, 0)))
SKIP4 = (
    (-1, (8, 4, 0)), (1, (7, 3, 0)), (-1, (7, 3, 0)), (1, (6, 2, 0)),
    (-1, (6, 2, 0)), (1, (5, 1, 0)), (-1, (5, 1, 0)), (1, (4, 0)),
)
CHAINS = (SKIP2, SKIP2, SKIP2, SKIP4)
ORDER = (
    ("m", 0), ("z", 0, 0), ("m", 1), ("z", 1, 0), ("k", 0), ("f", 2), ("s", 3), ("z", 0, 1), ("z", 1, 1),
    ("m", 2), ("z", 2, 0), ("k", 0), ("f", 3), ("z", 0, 2), ("m", 3), ("z", 3, 0), ("z", 1, 2), ("z", 2, 1),
    ("k", 0), ("z", 0, 3), ("z", 1, 3), ("z", 3, 1), ("z", 2, 2), ("e", 0), ("e", 1), ("z", 3, 2), ("z", 2, 3),
    ("z", 3, 3), ("e", 2), ("e", 3),
)
COUNTS = (("c", 1, 1, 0), ("x", 1, 2, 1), ("z", 1, 1, 0), ("z", 2, 4, 3))
COUNT_MSGS = sum(up + down for _, _, up, down in COUNTS)
SENDS, RECVS = 80, 80


def kernel(
    nz, slots, tok,
    gate_hbm, lift_hbm, cot_hbm, arrival, owner, mult, pieces,
    out,
    gate, lift, cot, in_sem,
    W, B, C, CT, H, HS, PR, ZS, ZR, CS, CR, R, FR,
    ssem, rsem,
):
    T = slots * tok
    nq = len(WIDTHS)
    half = sum(WIDTHS)
    offs = [sum(WIDTHS[:q]) for q in range(nq)]
    part = T // NY
    low, high = pl.ds(0, NX // 2), pl.ds(NX // 2, NX // 2)

    dp = lax.axis_index("dp")
    y = lax.axis_index("mp")
    x = dp // (NC * nz)
    z = (dp // NC) % nz
    c = dp % NC

    def dev(dx=0, dy=0, dz=0, flip=False):
        xx = (x + dx + NX) % NX
        yy = (y + dy + NY) % NY
        zz = (z + dz + nz) % nz
        cc = 1 - c if flip else c
        return (xx * (NC * nz) + zz * NC + cc, yy)

    sids, rids = iter(range(SENDS)), iter(range(RECVS))
    every = []

    def copy(src, dst, to, i, j):
        return pltpu.make_async_remote_copy(
            src_ref=src, dst_ref=dst, send_sem=ssem.at[i], recv_sem=rsem.at[j],
            device_id=to, device_id_type=MESH,
        )

    def send(src, dst, to):
        d = copy(src, dst, to, next(sids), next(rids))
        d.start()
        every.append(d)
        return d

    loads = [
        pltpu.make_async_copy(cot_hbm, cot, in_sem.at[0]),
        pltpu.make_async_copy(gate_hbm, gate, in_sem.at[1]),
        pltpu.make_async_copy(lift_hbm, lift, in_sem.at[2]),
    ]
    for d in loads:
        d.start()

    near = [dev(flip=True)] + [dev(dx=d) for d in (1, 2, 3)] + [dev(dy=d) for d in (1, 2, 3)]
    for h in (1, 2):
        near += [dev(dz=h), dev(dz=-h)]
    barrier = pltpu.get_barrier_semaphore()
    for n in near:
        pl.semaphore_signal(barrier, inc=1, device_id=n, device_id_type=MESH)
    pl.semaphore_wait(barrier, len(near))

    tiles = [pieces[owner[0, k]] for k in range(slots)]
    weights = [arrival[0] * mult[0, k] for k in range(slots)]
    count = sum(w * t for w, t in zip(weights, tiles)).astype(jnp.float32)

    loads[0].wait()
    token = lax.broadcasted_iota(jnp.int32, (part, 1), 0)
    for t in range(NY):
        scale = jnp.zeros((part, 1), jnp.float32)
        for k in range(slots):
            here = (token + t * part >= k * tok) & (token + t * part < (k + 1) * tok)
            scale = jnp.where(here, weights[k].astype(jnp.float32), scale)
        W[t] = (cot[pl.ds(t * part, part), :].astype(jnp.float32) * scale).astype(jnp.bfloat16)
    b_sent = [
        send(W.at[(y + d) % NY], B.at[NY - d], dev(dy=d)) for d in (2, 1, 3)
    ]
    B[0] = W[y]

    def count_rounds():
        total = jnp.full((8, 128), count, jnp.float32)
        slot = 0
        for kind, hop, up, down in COUNTS:
            last = [total, total]
            got = [None, None]
            for step in range(max(up, down) + 1):
                for side, (sign, n) in enumerate(((1, up), (-1, down))):
                    if 0 < step <= n:
                        d, at = got[side]
                        d.wait_recv()
                        last[side] = CR[at] + (total if step < n else 0.0)
                    if step < n:
                        CS[slot] = last[side]
                        to = {"c": dev(flip=True), "x": dev(dx=sign * hop), "z": dev(dz=sign * hop)}[kind]
                        got[side] = (send(CS.at[slot], CR.at[slot], to), slot)
                        slot += 1
                if step < max(up, down):
                    yield
            total = total + last[0]
            if down:
                total = total + last[1]
        CS[slot] = total

    rounds = count_rounds()

    def count_step():
        next(rounds, None)

    count_step()
    loads[1].wait()
    loads[2].wait()

    def hidden(k, which, q):
        rows = pl.ds(k * tok, tok)
        cols = pl.ds(pl.multiple_of(which * half + offs[q], 128), WIDTHS[q])
        g = gate[rows, cols].astype(jnp.float32)
        u = lift[rows, cols].astype(jnp.float32)
        h = g / (1.0 + jnp.exp(-g)) * u
        row = lax.broadcasted_iota(jnp.int32, h.shape, 0)
        return jnp.where(row < tiles[k] * TILE, h, 0.0).astype(jnp.bfloat16)

    h_core, h_up, h_dn, h_f = {}, {}, {}, {}

    def x_send(q, k):
        if k == 1:
            h_core[q].wait_recv()
        h_up[q, k] = send(H[q].at[0, k], H[q].at[3, k], dev(dx=1))
        h_dn[q, k] = send(H[q].at[0, k], H[q].at[1, k], dev(dx=-1))

    def forward(q):
        h_dn[q, 0].wait_recv()
        h_f[q, 0] = send(H[q].at[1, 0], H[q].at[2, 0], dev(dx=-1))
        h_up[q, 1].wait_recv()
        h_f[q, 1] = send(H[q].at[3, 1], H[q].at[2, 1], dev(dx=1))

    for q in range(nq):
        for k in range(slots):
            HS[q][pl.ds(k * tok, tok), :] = hidden(k, 1 - c, q)
        h_core[q] = send(HS[q], H[q].at[0, 1], dev(flip=True))
        for k in range(slots):
            H[q][0, 0, pl.ds(k * tok, tok), :] = hidden(k, c, q)
        if q == 0:
            x_send(0, 0)
            x_send(0, 1)

    for d in b_sent:
        d.wait_recv()
    c_sent = [
        send(B.at[(x + d + NY - y) % NY], C.at[0, y, NX - d], dev(dx=d)) for d in (2, 1, 3)
    ]
    C[0, y, 0] = B[(x + NY - y) % NY]
    count_step()
    forward(0)
    x_send(1, 0)
    x_send(1, 1)
    for d in c_sent:
        d.wait_recv()
    count_step()

    def pair(rs, sign):
        i, j = next(sids), next(rids)
        to = dev(dy=sign)
        out = copy(C.at[0, y, rs], C.at[0, y, rs], to, i, j)
        out.start()
        t = (y - sign + NY) % NY
        every.append(out)
        return copy(C.at[0, t, rs], C.at[0, t, rs], to, i, j)

    q_u1 = pair(high, 1)
    q_d1 = pair(low, -1)
    q_u2 = pair(low, 1)
    q_d2 = pair(high, -1)
    before, after, across = (y + NY - 1) % NY, (y + 1) % NY, (y + 2) % NY

    core = []

    def to_core(t):
        core.append(send(C.at[0, t], C.at[1, t], dev(flip=True)))

    to_core(y)
    x_send(2, 0)
    x_send(2, 1)
    q_u1.wait_recv()
    i, j = next(sids), next(rids)
    out_u = copy(C.at[0, before, high], C.at[0, before, high], dev(dy=1), i, j)
    in_u = copy(C.at[0, across, high], C.at[0, across, high], dev(dy=1), i, j)
    out_u.start()
    q_d1.wait_recv()
    i, j = next(sids), next(rids)
    out_d = copy(C.at[0, after, low], C.at[0, after, low], dev(dy=-1), i, j)
    in_d = copy(C.at[0, across, low], C.at[0, across, low], dev(dy=-1), i, j)
    out_d.start()
    every += [out_u, out_d]
    count_step()
    forward(1)
    q_u2.wait_recv()
    to_core(before)
    q_d2.wait_recv()
    to_core(after)
    count_step()
    in_u.wait_recv()
    in_d.wait_recv()
    to_core(across)
    for d in core:
        d.wait_recv()
    pieces_ = [C[k, t, r] for r in range(NX) for k in range(NC) for t in range(NY)]
    CT[...] = jnp.concatenate(pieces_, axis=0).T

    def active(q, s):
        return sum(len(dist) - 1 > s for _, dist in CHAINS[q])

    zsem = {
        (q, s): (next(sids), next(rids))
        for q in range(nq) for s in range(len(CHAINS[q][0][1]) - 1)
    }

    def z_wait(q, s, recv):
        n = active(q, s)
        d = copy(ZS[q].at[s, pl.ds(0, n)], ZR[q].at[s, pl.ds(0, n)], dev(dz=1), *zsem[q, s])
        d.wait_recv() if recv else d.wait_send()

    def product(q):
        for d in (h_up[q, 0], h_dn[q, 1], h_f[q, 0], h_f[q, 1]):
            d.wait_recv()
        rhs = H[q][...].reshape(NX * NC * T, WIDTHS[q])
        for m in range(4):
            acc = jnp.dot(CT[pl.ds(m * 128, 128), :], rhs, preferred_element_type=jnp.float32)
            PR[q][pl.ds(m * (nz // 4), nz // 4)] = acc.reshape(nz // 4, 128 * 4 // nz, WIDTHS[q])

    def z_step(q, s):
        if s > 0:
            z_wait(q, s - 1, True)
        for ci in range(active(q, s)):
            sign, dist = CHAINS[q][ci]
            v = PR[q][(z + sign * dist[s] + nz) % nz]
            if s > 0:
                v = v + ZR[q][s - 1, ci].astype(jnp.float32)
            ZS[q][s, ci] = v.astype(jnp.bfloat16)
            to = dev(dz=sign * (dist[s] - dist[s + 1]))
            copy(ZS[q].at[s, ci], ZR[q].at[s, ci], to, *zsem[q, s]).start()

    fin = {}

    def end(q):
        for _ in rounds:
            pass
        steps = len(CHAINS[q][0][1]) - 1
        z_wait(q, steps - 1, True)
        v = PR[q][z]
        for ci, (_, dist) in enumerate(CHAINS[q]):
            v = v + ZR[q][len(dist) - 2, ci].astype(jnp.float32)
        total = CS[COUNT_MSGS][0:1, 0:1] * float(TILE)
        R[q][...] = (v / total).reshape(R[q].shape)
        fin[q] = send(R[q].at[1 - c], FR[q], dev(flip=True))
        out[:, pl.ds(pl.multiple_of(c * half + offs[q], 128), WIDTHS[q])] = R[q][c]

    for event in ORDER:
        q = event[1]
        if event[0] == "s":
            x_send(q, 0)
            x_send(q, 1)
        elif event[0] == "k":
            count_step()
        elif event[0] == "f":
            forward(q)
        elif event[0] == "m":
            product(q)
        elif event[0] == "z":
            if event[2] < len(CHAINS[q][0][1]) - 1:
                z_step(q, event[2])
        else:
            end(q)
    for q in range(nq):
        fin[q].wait_recv()
        out[:, pl.ds(pl.multiple_of((1 - c) * half + offs[q], 128), WIDTHS[q])] = FR[q][...]
    for d in every:
        d.wait_send()
    for q, s in zsem:
        z_wait(q, s, False)


def on_device(nz, gate, lift, cot, arrival, owner, mult, pieces):
    _, slots, tok, ff = gate.shape
    db = cot.shape[3]
    T = slots * tok
    rows = db // nz
    bf, f32 = jnp.bfloat16, jnp.float32
    V = pltpu.VMEM
    any_ = pl.BlockSpec(memory_space=pl.ANY)
    smem = pl.BlockSpec(memory_space=pltpu.SMEM)
    zbuf = [V((len(ch[0][1]) - 1, len(ch), rows, w), bf) for ch, w in zip(CHAINS, WIDTHS)]
    n = COUNT_MSGS
    return pl.pallas_call(
        functools.partial(kernel, nz, slots, tok),
        out_shape=jax.ShapeDtypeStruct((rows // NC, ff), f32),
        in_specs=[any_, any_, any_, smem, smem, smem, smem],
        out_specs=pl.BlockSpec(memory_space=pltpu.VMEM),
        scratch_shapes=[
            V((T, ff), bf), V((T, ff), bf), V((T, db), bf), pltpu.SemaphoreType.DMA((3,)),
            V((NY, T // NY, db), bf), V((NY, T // NY, db), bf),
            V((NC, NY, NX, T // NY, db), bf), V((db, NX * NC * T), bf),
            [V((NX, NC, T, w), bf) for w in WIDTHS],
            [V((T, w), bf) for w in WIDTHS],
            [V((nz, rows, w), f32) for w in WIDTHS],
            zbuf, list(zbuf),
            V((n + 1, 8, 128), f32), V((n, 8, 128), f32),
            [V((NC, rows // NC, w), f32) for w in WIDTHS],
            [V((rows // NC, w), f32) for w in WIDTHS],
            pltpu.SemaphoreType.DMA((SENDS,)), pltpu.SemaphoreType.DMA((RECVS,)),
        ],
        compiler_params=pltpu.CompilerParams(
            collective_id=0, has_side_effects=True, vmem_limit_bytes=60 * 1024 * 1024
        ),
    )(
        gate.reshape(T, ff), lift.reshape(T, ff), cot.reshape(T, db),
        arrival, owner, mult, pieces,
    )


def solution(mesh):
    nz = mesh.shape["dp"] // (NX * NC)
    return jax.shard_map(
        functools.partial(on_device, nz),
        mesh=mesh,
        in_specs=(
            P("dp", None, None, "mp"),
            P("dp", None, None, "mp"),
            P("dp", None, None, "mp"),
            P("dp"),
            P("dp", None),
            P("dp", None),
            P(),
        ),
        out_specs=P("dp", "mp"),
        check_vma=False,
    )
```

time: 99.2 us -> 69.4 us (0.70)
  Pallas kernels: 96.8 us -> 67 us
    pallas_call x1, Pallas kernels: 96.8 us -> 67 us  [on_device(): pl.pallas_call(functools.partial(kernel, nz, slots, tok), out_shape=jax.S...]
where the time goes in v2:
time: 69.4 us; the launch traced here: 69.3 us
  Pallas kernels  67 us (97%)
  local copies, waits for them, and re-layouts  1.55 us (2%)
    pallas_call x1, Pallas kernels, on_device(): pl.pallas_call(functools.partial(kernel, nz, slots, tok), out_shape=jax.S...  67 us
    unnamed x1, local copies, waits for them, and re-layouts  1.55 us

profile of v2, /device:TPU:1, one launch (start us, length us, event | category | flops | bytes accessed | tf_op | source)
XLA Modules:
  0.0 69.3 jit_solution(18101178375869720122)
XLA Ops:
  0.7 67.0 %shard_map.73 = f32[16,1792]{1,0:T(8,128)} custom-call(bf16[192,1792]{1,0:T(8,128)(2,1)} %bitcast.3, bf16[192,1792]{1,0:T(8,128)(2,1)} %bitcast.4, bf16[192,512]{1,0:T(8,128)(2,1)} %bitcast.5, s32[1]{0:T(128)S(6)} %copy.9.arrival, s32[1,3]{1,0:T(1,128)} %owner.1, s32[1,3]{1,0:T(1,128)} %mult.1, s32[128]{0:T(128)} %pieces.1), custom_call_target="tpu_custom_call" | custom-call | tf_op jit(solution)/shard_map/pallas_call | solution.py:322
  67.7 1.6 %copy.10 = f32[16,1792]{1,0:T(8,128)} copy(f32[16,1792]{1,0:T(8,128)} %shard_map.73) | data formatting | bytes 229376

commit v3 on v2

--- a/solution.py
+++ b/solution.py
@@ -13,17 +13,20 @@
 NY = 4
 NC = 2
 WIDTHS = (256, 256, 256, 128)
-SKIP2 = ((-1, (8, 6, 4, 2, 0)), (1, (7, 5, 3, 1, 0)), (-1, (7, 5, 3, 1, 0)), (1, (6, 4, 2, 0)))
-SKIP4 = (
-    (-1, (8, 4, 0)), (1, (7, 3, 0)), (-1, (7, 3, 0)), (1, (6, 2, 0)),
-    (-1, (6, 2, 0)), (1, (5, 1, 0)), (-1, (5, 1, 0)), (1, (4, 0)),
+BOTH = (1, -1)
+LEAVES = tuple((g, d, d - 1) for d in (7, 5, 3, 1) for g in BOTH)
+TREE2 = (
+    (0, LEAVES), (0, ((-1, 8, 6),)), (1, ((1, 6, 4), (-1, 6, 4))), (2, ((1, 4, 2), (-1, 4, 2))),
+    (3, ((1, 2, 0), (-1, 2, 0))),
 )
-CHAINS = (SKIP2, SKIP2, SKIP2, SKIP4)
+TREE4 = (
+    (0, LEAVES), (0, ((-1, 8, 4),)), (1, ((1, 6, 4), (-1, 6, 4), (1, 2, 0), (-1, 2, 0))), (2, ((1, 4, 0), (-1, 4, 0))),
+)
+TREES = (TREE2, TREE2, TREE4, TREE4)
 ORDER = (
-    ("m", 0), ("z", 0, 0), ("m", 1), ("z", 1, 0), ("k", 0), ("f", 2), ("s", 3), ("z", 0, 1), ("z", 1, 1),
-    ("m", 2), ("z", 2, 0), ("k", 0), ("f", 3), ("z", 0, 2), ("m", 3), ("z", 3, 0), ("z", 1, 2), ("z", 2, 1),
-    ("k", 0), ("z", 0, 3), ("z", 1, 3), ("z", 3, 1), ("z", 2, 2), ("e", 0), ("e", 1), ("z", 3, 2), ("z", 2, 3),
-    ("z", 3, 3), ("e", 2), ("e", 3),
+    ("m", 0), ("z", 0, 0), ("f", 2), ("k", 0), ("m", 1), ("z", 1, 0), ("z", 0, 1), ("f", 3), ("z", 0, 2), ("k", 0),
+    ("z", 1, 1), ("m", 2), ("z", 2, 0), ("m", 3), ("z", 3, 0), ("k", 0), ("z", 0, 3), ("z", 2, 1), ("z", 1, 2),
+    ("z", 3, 1), ("e", 0), ("z", 2, 2), ("z", 1, 3), ("z", 3, 2), ("e", 1), ("e", 2), ("e", 3),
 )
 COUNTS = (("c", 1, 1, 0), ("x", 1, 2, 1), ("z", 1, 1, 0), ("z", 2, 4, 3))
 COUNT_MSGS = sum(up + down for _, _, up, down in COUNTS)
@@ -35,7 +38,7 @@
     gate_hbm, lift_hbm, cot_hbm, arrival, owner, mult, pieces,
     out,
     gate, lift, cot, in_sem,
-    W, B, C, CT, H, HS, PR, ZS, ZR, CS, CR, R, FR,
+    W, B, C, CT, H, HS, PR, ZS, ZR, CS, CR, R, out_sem,
     ssem, rsem,
 ):
     T = slots * tok
@@ -222,6 +225,8 @@
     every += [out_u, out_d]
     count_step()
     forward(1)
+    x_send(3, 0)
+    x_send(3, 1)
     q_u2.wait_recv()
     to_core(before)
     q_d2.wait_recv()
@@ -235,18 +240,29 @@
     pieces_ = [C[k, t, r] for r in range(NX) for k in range(NC) for t in range(NY)]
     CT[...] = jnp.concatenate(pieces_, axis=0).T
 
-    def active(q, s):
-        return sum(len(dist) - 1 > s for _, dist in CHAINS[q])
-
-    zsem = {
-        (q, s): (next(sids), next(rids))
-        for q in range(nq) for s in range(len(CHAINS[q][0][1]) - 1)
-    }
-
-    def z_wait(q, s, recv):
-        n = active(q, s)
-        d = copy(ZS[q].at[s, pl.ds(0, n)], ZR[q].at[s, pl.ds(0, n)], dev(dz=1), *zsem[q, s])
-        d.wait_recv() if recv else d.wait_send()
+    zsem = {(q, g): (next(sids), next(rids)) for q in range(nq) for g in range(len(TREES[q]))}
+    first = {}
+    for q in range(nq):
+        n = 0
+        for g, (_, group) in enumerate(TREES[q]):
+            first[q, g] = n
+            n += len(group)
+    waited = set()
+
+    def z_group(q, g):
+        at = pl.ds(first[q, g], len(TREES[q][g][1]))
+        return copy(ZS[q].at[at], ZR[q].at[at], dev(dz=1), *zsem[q, g])
+
+    def z_sum(q, sign, dist):
+        v = PR[q][(z + sign * dist + nz) % nz]
+        for g, (_, group) in enumerate(TREES[q]):
+            for i, (way, _, to) in enumerate(group):
+                if to == dist and (way == sign or dist == 0):
+                    if (q, g) not in waited:
+                        waited.add((q, g))
+                        z_group(q, g).wait_recv()
+                    v = v + ZR[q][first[q, g] + i].astype(jnp.float32)
+        return v
 
     def product(q):
         for d in (h_up[q, 0], h_dn[q, 1], h_f[q, 0], h_f[q, 1]):
@@ -257,31 +273,30 @@
             PR[q][pl.ds(m * (nz // 4), nz // 4)] = acc.reshape(nz // 4, 128 * 4 // nz, WIDTHS[q])
 
     def z_step(q, s):
-        if s > 0:
-            z_wait(q, s - 1, True)
-        for ci in range(active(q, s)):
-            sign, dist = CHAINS[q][ci]
-            v = PR[q][(z + sign * dist[s] + nz) % nz]
-            if s > 0:
-                v = v + ZR[q][s - 1, ci].astype(jnp.float32)
-            ZS[q][s, ci] = v.astype(jnp.bfloat16)
-            to = dev(dz=sign * (dist[s] - dist[s + 1]))
-            copy(ZS[q].at[s, ci], ZR[q].at[s, ci], to, *zsem[q, s]).start()
-
-    fin = {}
+        for g, (step, group) in enumerate(TREES[q]):
+            if step == s:
+                for i, (sign, dist, to) in enumerate(group):
+                    slot = first[q, g] + i
+                    ZS[q][slot] = z_sum(q, sign, dist).astype(jnp.bfloat16)
+                    copy(ZS[q].at[slot], ZR[q].at[slot], dev(dz=sign * (dist - to)), *zsem[q, g]).start()
+
+    fin = []
 
     def end(q):
         for _ in rounds:
             pass
-        steps = len(CHAINS[q][0][1]) - 1
-        z_wait(q, steps - 1, True)
-        v = PR[q][z]
-        for ci, (_, dist) in enumerate(CHAINS[q]):
-            v = v + ZR[q][len(dist) - 2, ci].astype(jnp.float32)
         total = CS[COUNT_MSGS][0:1, 0:1] * float(TILE)
-        R[q][...] = (v / total).reshape(R[q].shape)
-        fin[q] = send(R[q].at[1 - c], FR[q], dev(flip=True))
-        out[:, pl.ds(pl.multiple_of(c * half + offs[q], 128), WIDTHS[q])] = R[q][c]
+        R[q][...] = (z_sum(q, 1, 0) / total).reshape(R[q].shape)
+        cols = out.at[:, pl.ds(pl.multiple_of(c * half + offs[q], 128), WIDTHS[q])]
+        theirs = out.at[:, pl.ds(pl.multiple_of((1 - c) * half + offs[q], 128), WIDTHS[q])]
+        i, j = next(sids), next(rids)
+        d = copy(R[q].at[1 - c], cols, dev(flip=True), i, j)
+        d.start()
+        every.append(d)
+        fin.append(copy(R[q].at[1 - c], theirs, dev(flip=True), i, j).wait_recv)
+        d = pltpu.make_async_copy(R[q].at[c], cols, out_sem.at[q])
+        d.start()
+        fin.append(d.wait)
 
     for event in ORDER:
         q = event[1]
@@ -295,17 +310,15 @@
         elif event[0] == "m":
             product(q)
         elif event[0] == "z":
-            if event[2] < len(CHAINS[q][0][1]) - 1:
-                z_step(q, event[2])
+            z_step(q, event[2])
         else:
             end(q)
-    for q in range(nq):
-        fin[q].wait_recv()
-        out[:, pl.ds(pl.multiple_of((1 - c) * half + offs[q], 128), WIDTHS[q])] = FR[q][...]
+    for wait in fin:
+        wait()
     for d in every:
         d.wait_send()
-    for q, s in zsem:
-        z_wait(q, s, False)
+    for q, g in zsem:
+        z_group(q, g).wait_send()
 
 
 def on_device(nz, gate, lift, cot, arrival, owner, mult, pieces):
@@ -317,13 +330,13 @@
     V = pltpu.VMEM
     any_ = pl.BlockSpec(memory_space=pl.ANY)
     smem = pl.BlockSpec(memory_space=pltpu.SMEM)
-    zbuf = [V((len(ch[0][1]) - 1, len(ch), rows, w), bf) for ch, w in zip(CHAINS, WIDTHS)]
+    zbuf = [V((sum(len(g) for _, g in tree), rows, w), bf) for tree, w in zip(TREES, WIDTHS)]
     n = COUNT_MSGS
     return pl.pallas_call(
         functools.partial(kernel, nz, slots, tok),
         out_shape=jax.ShapeDtypeStruct((rows // NC, ff), f32),
         in_specs=[any_, any_, any_, smem, smem, smem, smem],
-        out_specs=pl.BlockSpec(memory_space=pltpu.VMEM),
+        out_specs=any_,
         scratch_shapes=[
             V((T, ff), bf), V((T, ff), bf), V((T, db), bf), pltpu.SemaphoreType.DMA((3,)),
             V((NY, T // NY, db), bf), V((NY, T // NY, db), bf),
@@ -334,7 +347,7 @@
             zbuf, list(zbuf),
             V((n + 1, 8, 128), f32), V((n, 8, 128), f32),
             [V((NC, rows // NC, w), f32) for w in WIDTHS],
-            [V((rows // NC, w), f32) for w in WIDTHS],
+            pltpu.SemaphoreType.DMA((len(WIDTHS),)),
             pltpu.SemaphoreType.DMA((SENDS,)), pltpu.SemaphoreType.DMA((RECVS,)),
         ],
         compiler_params=pltpu.CompilerParams(

time: 69.4 us -> 65.3 us (0.941)
  Pallas kernels: 67 us -> 62.9 us
    pallas_call x1, Pallas kernels: 67 us -> 62.9 us  [on_device(): pl.pallas_call(functools.partial(kernel, nz, slots, tok), out_shape=jax.S...]
where the time goes in v3:
time: 65.3 us; the launch traced here: 65.1 us
  Pallas kernels  62.9 us (96%)
  local copies, waits for them, and re-layouts  1.55 us (2%)
  between operations  0.66 us (1%)
    pallas_call x1, Pallas kernels, on_device(): pl.pallas_call(functools.partial(kernel, nz, slots, tok), out_shape=jax.S...  62.9 us
    unnamed x1, local copies, waits for them, and re-layouts  1.55 us

profile of v3, /device:TPU:1, one launch (start us, length us, event | category | flops | bytes accessed | tf_op | source)
XLA Modules:
  0.0 65.1 jit_solution(8602687236761292646)
XLA Ops:
  0.7 62.9 %shard_map.73 = f32[16,1792]{1,0:T(8,128)} custom-call(bf16[192,1792]{1,0:T(8,128)(2,1)} %bitcast.3, bf16[192,1792]{1,0:T(8,128)(2,1)} %bitcast.4, bf16[192,512]{1,0:T(8,128)(2,1)} %bitcast.5, s32[1]{0:T(128)S(6)} %copy.9.arrival, s32[1,3]{1,0:T(1,128)} %owner.1, s32[1,3]{1,0:T(1,128)} %mult.1, s32[128]{0:T(128)} %pieces.1), custom_call_target="tpu_custom_call" | custom-call | tf_op jit(solution)/shard_map/pallas_call | solution.py:335
  63.6 1.6 %copy.10 = f32[16,1792]{1,0:T(8,128)} copy(f32[16,1792]{1,0:T(8,128)} %shard_map.73) | data formatting | bytes 229376

commit v4 on v3

--- a/solution.py
+++ b/solution.py
@@ -53,6 +53,7 @@
     x = dp // (NC * nz)
     z = (dp // NC) % nz
     c = dp % NC
+    turn = 1 - 2 * c
 
     def dev(dx=0, dy=0, dz=0, flip=False):
         xx = (x + dx + NX) % NX
@@ -254,7 +255,7 @@
         return copy(ZS[q].at[at], ZR[q].at[at], dev(dz=1), *zsem[q, g])
 
     def z_sum(q, sign, dist):
-        v = PR[q][(z + sign * dist + nz) % nz]
+        v = PR[q][(z + turn * sign * dist + nz) % nz]
         for g, (_, group) in enumerate(TREES[q]):
             for i, (way, _, to) in enumerate(group):
                 if to == dist and (way == sign or dist == 0):
@@ -278,7 +279,7 @@
                 for i, (sign, dist, to) in enumerate(group):
                     slot = first[q, g] + i
                     ZS[q][slot] = z_sum(q, sign, dist).astype(jnp.bfloat16)
-                    copy(ZS[q].at[slot], ZR[q].at[slot], dev(dz=sign * (dist - to)), *zsem[q, g]).start()
+                    copy(ZS[q].at[slot], ZR[q].at[slot], dev(dz=turn * sign * (dist - to)), *zsem[q, g]).start()
 
     fin = []
 

time: 65.3 us -> 64.7 us (level)
  no operation moved by 1% of the time
where the time goes in v4:
time: 64.7 us; the launch traced here: 64.6 us
  Pallas kernels  62.4 us (96%)
  local copies, waits for them, and re-layouts  1.55 us (2%)
  between operations  0.66 us (1%)
    pallas_call x1, Pallas kernels, on_device(): pl.pallas_call(functools.partial(kernel, nz, slots, tok), out_shape=jax.S...  62.4 us
    unnamed x1, local copies, waits for them, and re-layouts  1.55 us

profile of v4, /device:TPU:1, one launch (start us, length us, event | category | flops | bytes accessed | tf_op | source)
XLA Modules:
  0.0 64.6 jit_solution(964817895666504695)
XLA Ops:
  0.7 62.4 %shard_map.73 = f32[16,1792]{1,0:T(8,128)} custom-call(bf16[192,1792]{1,0:T(8,128)(2,1)} %bitcast.3, bf16[192,1792]{1,0:T(8,128)(2,1)} %bitcast.4, bf16[192,512]{1,0:T(8,128)(2,1)} %bitcast.5, s32[1]{0:T(128)S(6)} %copy.9.arrival, s32[1,3]{1,0:T(1,128)} %owner.1, s32[1,3]{1,0:T(1,128)} %mult.1, s32[128]{0:T(128)} %pieces.1), custom_call_target="tpu_custom_call" | custom-call | tf_op jit(solution)/shard_map/pallas_call | solution.py:336
  63.0 1.6 %copy.10 = f32[16,1792]{1,0:T(8,128)} copy(f32[16,1792]{1,0:T(8,128)} %shard_map.73) | data formatting | bytes 229376

commit v5 on v4

--- a/solution.py
+++ b/solution.py
@@ -30,14 +30,14 @@
 )
 COUNTS = (("c", 1, 1, 0), ("x", 1, 2, 1), ("z", 1, 1, 0), ("z", 2, 4, 3))
 COUNT_MSGS = sum(up + down for _, _, up, down in COUNTS)
-SENDS, RECVS = 80, 80
+SENDS, RECVS = 21, 59
 
 
 def kernel(
     nz, slots, tok,
-    gate_hbm, lift_hbm, cot_hbm, arrival, owner, mult, pieces,
+    gate_hbm, lift_hbm, cot_hbm, arrival_hbm, owner_hbm, mult_hbm, pieces_hbm,
     out,
-    gate, lift, cot, in_sem,
+    gate, lift, cot, arrival, owner, mult, pieces, in_sem,
     W, B, C, CT, H, HS, PR, ZS, ZR, CS, CR, R, out_sem,
     ssem, rsem,
 ):
@@ -71,16 +71,32 @@
             device_id=to, device_id_type=MESH,
         )
 
-    def send(src, dst, to):
-        d = copy(src, dst, to, next(sids), next(rids))
+    def send(src, dst, to, i=None, j=None):
+        if i is None:
+            i = next(sids)
+            own = True
+        else:
+            own = False
+        d = copy(src, dst, to, i, next(rids) if j is None else j)
         d.start()
-        every.append(d)
+        if own:
+            every.append(d)
         return d
+
+    s_count, s_b, s_c, s_quarter, s_core = (next(sids) for _ in range(5))
+    s_h = [next(sids) for _ in range(nq)]
+    s_z = [next(sids) for _ in range(nq)]
+    r_b, r_c, r_core = (next(rids) for _ in range(3))
+    r_h = [next(rids) for _ in range(nq)]
 
     loads = [
         pltpu.make_async_copy(cot_hbm, cot, in_sem.at[0]),
         pltpu.make_async_copy(gate_hbm, gate, in_sem.at[1]),
         pltpu.make_async_copy(lift_hbm, lift, in_sem.at[2]),
+        pltpu.make_async_copy(arrival_hbm, arrival, in_sem.at[3]),
+        pltpu.make_async_copy(owner_hbm, owner, in_sem.at[4]),
+        pltpu.make_async_copy(mult_hbm, mult, in_sem.at[5]),
+        pltpu.make_async_copy(pieces_hbm, pieces, in_sem.at[6]),
     ]
     for d in loads:
         d.start()
@@ -93,6 +109,8 @@
         pl.semaphore_signal(barrier, inc=1, device_id=n, device_id_type=MESH)
     pl.semaphore_wait(barrier, len(near))
 
+    for d in loads[3:]:
+        d.wait()
     tiles = [pieces[owner[0, k]] for k in range(slots)]
     weights = [arrival[0] * mult[0, k] for k in range(slots)]
     count = sum(w * t for w, t in zip(weights, tiles)).astype(jnp.float32)
@@ -105,9 +123,8 @@
             here = (token + t * part >= k * tok) & (token + t * part < (k + 1) * tok)
             scale = jnp.where(here, weights[k].astype(jnp.float32), scale)
         W[t] = (cot[pl.ds(t * part, part), :].astype(jnp.float32) * scale).astype(jnp.bfloat16)
-    b_sent = [
-        send(W.at[(y + d) % NY], B.at[NY - d], dev(dy=d)) for d in (2, 1, 3)
-    ]
+    for d in (2, 1, 3):
+        send(W.at[(y + d) % NY], B.at[NY - d], dev(dy=d), s_b, r_b)
     B[0] = W[y]
 
     def count_rounds():
@@ -125,7 +142,7 @@
                     if step < n:
                         CS[slot] = last[side]
                         to = {"c": dev(flip=True), "x": dev(dx=sign * hop), "z": dev(dz=sign * hop)}[kind]
-                        got[side] = (send(CS.at[slot], CR.at[slot], to), slot)
+                        got[side] = (send(CS.at[slot], CR.at[slot], to, s_count), slot)
                         slot += 1
                 if step < max(up, down):
                     yield
@@ -152,19 +169,19 @@
         row = lax.broadcasted_iota(jnp.int32, h.shape, 0)
         return jnp.where(row < tiles[k] * TILE, h, 0.0).astype(jnp.bfloat16)
 
-    h_core, h_up, h_dn, h_f = {}, {}, {}, {}
+    h_core, h_up, h_dn = {}, {}, {}
 
     def x_send(q, k):
         if k == 1:
             h_core[q].wait_recv()
-        h_up[q, k] = send(H[q].at[0, k], H[q].at[3, k], dev(dx=1))
-        h_dn[q, k] = send(H[q].at[0, k], H[q].at[1, k], dev(dx=-1))
+        h_up[q, k] = send(H[q].at[0, k], H[q].at[3, k], dev(dx=1), s_h[q], r_h[q] if k == 0 else None)
+        h_dn[q, k] = send(H[q].at[0, k], H[q].at[1, k], dev(dx=-1), s_h[q], r_h[q] if k == 1 else None)
 
     def forward(q):
         h_dn[q, 0].wait_recv()
-        h_f[q, 0] = send(H[q].at[1, 0], H[q].at[2, 0], dev(dx=-1))
+        send(H[q].at[1, 0], H[q].at[2, 0], dev(dx=-1), s_h[q], r_h[q])
         h_up[q, 1].wait_recv()
-        h_f[q, 1] = send(H[q].at[3, 1], H[q].at[2, 1], dev(dx=1))
+        send(H[q].at[3, 1], H[q].at[2, 1], dev(dx=1), s_h[q], r_h[q])
 
     for q in range(nq):
         for k in range(slots):
@@ -176,27 +193,23 @@
             x_send(0, 0)
             x_send(0, 1)
 
-    for d in b_sent:
-        d.wait_recv()
-    c_sent = [
-        send(B.at[(x + d + NY - y) % NY], C.at[0, y, NX - d], dev(dx=d)) for d in (2, 1, 3)
-    ]
+    copy(B.at[pl.ds(1, 3)], B.at[pl.ds(1, 3)], dev(dy=1), s_b, r_b).wait_recv()
+    for d in (2, 1, 3):
+        send(B.at[(x + d + NY - y) % NY], C.at[0, y, NX - d], dev(dx=d), s_c, r_c)
     C[0, y, 0] = B[(x + NY - y) % NY]
     count_step()
     forward(0)
     x_send(1, 0)
     x_send(1, 1)
-    for d in c_sent:
-        d.wait_recv()
+    copy(B.at[pl.ds(1, 3)], C.at[0, y, pl.ds(1, 3)], dev(dx=1), s_c, r_c).wait_recv()
     count_step()
 
     def pair(rs, sign):
-        i, j = next(sids), next(rids)
+        i, j = s_quarter, next(rids)
         to = dev(dy=sign)
         out = copy(C.at[0, y, rs], C.at[0, y, rs], to, i, j)
         out.start()
         t = (y - sign + NY) % NY
-        every.append(out)
         return copy(C.at[0, t, rs], C.at[0, t, rs], to, i, j)
 
     q_u1 = pair(high, 1)
@@ -205,25 +218,22 @@
     q_d2 = pair(high, -1)
     before, after, across = (y + NY - 1) % NY, (y + 1) % NY, (y + 2) % NY
 
-    core = []
-
     def to_core(t):
-        core.append(send(C.at[0, t], C.at[1, t], dev(flip=True)))
+        send(C.at[0, t], C.at[1, t], dev(flip=True), s_core, r_core)
 
     to_core(y)
     x_send(2, 0)
     x_send(2, 1)
     q_u1.wait_recv()
-    i, j = next(sids), next(rids)
+    i, j = s_quarter, next(rids)
     out_u = copy(C.at[0, before, high], C.at[0, before, high], dev(dy=1), i, j)
     in_u = copy(C.at[0, across, high], C.at[0, across, high], dev(dy=1), i, j)
     out_u.start()
     q_d1.wait_recv()
-    i, j = next(sids), next(rids)
+    i, j = s_quarter, next(rids)
     out_d = copy(C.at[0, after, low], C.at[0, after, low], dev(dy=-1), i, j)
     in_d = copy(C.at[0, across, low], C.at[0, across, low], dev(dy=-1), i, j)
     out_d.start()
-    every += [out_u, out_d]
     count_step()
     forward(1)
     x_send(3, 0)
@@ -236,12 +246,11 @@
     in_u.wait_recv()
     in_d.wait_recv()
     to_core(across)
-    for d in core:
-        d.wait_recv()
+    copy(C.at[0], C.at[1], dev(flip=True), s_core, r_core).wait_recv()
     pieces_ = [C[k, t, r] for r in range(NX) for k in range(NC) for t in range(NY)]
     CT[...] = jnp.concatenate(pieces_, axis=0).T
 
-    zsem = {(q, g): (next(sids), next(rids)) for q in range(nq) for g in range(len(TREES[q]))}
+    zsem = {(q, g): (s_z[q], next(rids)) for q in range(nq) for g in range(len(TREES[q]))}
     first = {}
     for q in range(nq):
         n = 0
@@ -266,8 +275,8 @@
         return v
 
     def product(q):
-        for d in (h_up[q, 0], h_dn[q, 1], h_f[q, 0], h_f[q, 1]):
-            d.wait_recv()
+        four = H[q].at[pl.ds(2, 2)]
+        copy(four, four, dev(dx=1), s_h[q], r_h[q]).wait_recv()
         rhs = H[q][...].reshape(NX * NC * T, WIDTHS[q])
         for m in range(4):
             acc = jnp.dot(CT[pl.ds(m * 128, 128), :], rhs, preferred_element_type=jnp.float32)
@@ -318,8 +327,12 @@
         wait()
     for d in every:
         d.wait_send()
-    for q, g in zsem:
-        z_group(q, g).wait_send()
+    groups = [(s_count, CS.at[pl.ds(0, COUNT_MSGS)]), (s_b, B.at[pl.ds(0, 3)]), (s_c, B.at[pl.ds(0, 3)])]
+    groups += [(s_quarter, C.at[0, pl.ds(0, 3)]), (s_core, C.at[0])]
+    for q in range(nq):
+        groups += [(s_h[q], H[q].at[pl.ds(0, 3)]), (s_z[q], ZS[q])]
+    for i, ref in groups:
+        copy(ref, ref, dev(dx=1), i, r_b).wait_send()
 
 
 def on_device(nz, gate, lift, cot, arrival, owner, mult, pieces):
@@ -330,16 +343,16 @@
     bf, f32 = jnp.bfloat16, jnp.float32
     V = pltpu.VMEM
     any_ = pl.BlockSpec(memory_space=pl.ANY)
-    smem = pl.BlockSpec(memory_space=pltpu.SMEM)
     zbuf = [V((sum(len(g) for _, g in tree), rows, w), bf) for tree, w in zip(TREES, WIDTHS)]
     n = COUNT_MSGS
     return pl.pallas_call(
         functools.partial(kernel, nz, slots, tok),
         out_shape=jax.ShapeDtypeStruct((rows // NC, ff), f32),
-        in_specs=[any_, any_, any_, smem, smem, smem, smem],
+        in_specs=[any_] * 7,
         out_specs=any_,
         scratch_shapes=[
-            V((T, ff), bf), V((T, ff), bf), V((T, db), bf), pltpu.SemaphoreType.DMA((3,)),
+            V((T, ff), bf), V((T, ff), bf), V((T, db), bf),
+            *(pltpu.SMEM(a.shape, jnp.int32) for a in (arrival, owner, mult, pieces)), pltpu.SemaphoreType.DMA((7,)),
             V((NY, T // NY, db), bf), V((NY, T // NY, db), bf),
             V((NC, NY, NX, T // NY, db), bf), V((db, NX * NC * T), bf),
             [V((NX, NC, T, w), bf) for w in WIDTHS],

time: 64.7 us -> 63.3 us (0.978)
  Pallas kernels: 62.4 us -> 61 us
    pallas_call x1, Pallas kernels: 62.4 us -> 61 us  [on_device(): pl.pallas_call(functools.partial(kernel, nz, slots, tok), out_shape=jax.S...]
where the time goes in v5:
time: 63.3 us; the launch traced here: 63.2 us
  Pallas kernels  61 us (96%)
  local copies, waits for them, and re-layouts  1.55 us (2%)
  between operations  0.66 us (1%)
    pallas_call x1, Pallas kernels, on_device(): pl.pallas_call(functools.partial(kernel, nz, slots, tok), out_shape=jax.S...  61 us
    unnamed x1, local copies, waits for them, and re-layouts  1.55 us

profile of v5, /device:TPU:1, one launch (start us, length us, event | category | flops | bytes accessed | tf_op | source)
XLA Modules:
  0.0 63.2 jit_solution(15738883880082611300)
XLA Ops:
  0.7 61.0 %shard_map.73 = f32[16,1792]{1,0:T(8,128)} custom-call(bf16[192,1792]{1,0:T(8,128)(2,1)} %bitcast.3, bf16[192,1792]{1,0:T(8,128)(2,1)} %bitcast.4, bf16[192,512]{1,0:T(8,128)(2,1)} %bitcast.5, s32[1]{0:T(128)S(6)} %copy.9.arrival_hbm, s32[1,3]{1,0:T(1,128)} %owner_hbm.1, s32[1,3]{1,0:T(1,128)} %mult_hbm.1, s32[128]{0:T(128)} %pieces_hbm.1), custom_call_target="tpu_custom_call" | custom-call | tf_op jit(solution)/shard_map/pallas_call | solution.py:348
  61.6 1.6 %copy.10 = f32[16,1792]{1,0:T(8,128)} copy(f32[16,1792]{1,0:T(8,128)} %shard_map.73) | data formatting | bytes 229376

commit v6 on v5

--- a/solution.py
+++ b/solution.py
@@ -24,9 +24,9 @@
 )
 TREES = (TREE2, TREE2, TREE4, TREE4)
 ORDER = (
-    ("m", 0), ("z", 0, 0), ("f", 2), ("k", 0), ("m", 1), ("z", 1, 0), ("z", 0, 1), ("f", 3), ("z", 0, 2), ("k", 0),
-    ("z", 1, 1), ("m", 2), ("z", 2, 0), ("m", 3), ("z", 3, 0), ("k", 0), ("z", 0, 3), ("z", 2, 1), ("z", 1, 2),
-    ("z", 3, 1), ("e", 0), ("z", 2, 2), ("z", 1, 3), ("z", 3, 2), ("e", 1), ("e", 2), ("e", 3),
+    ("m", 0), ("z", 0, 0), ("f", 2), ("k", 0), ("m", 1), ("z", 1, 0), ("f", 3), ("z", 0, 1), ("k", 0),
+    ("m", 2), ("z", 2, 0), ("z", 1, 1), ("z", 0, 2), ("m", 3), ("z", 3, 0), ("z", 2, 1), ("z", 1, 2), ("z", 3, 1),
+    ("z", 2, 2), ("k", 0), ("z", 0, 3), ("z", 3, 2), ("z", 1, 3), ("e", 0), ("e", 1), ("e", 2), ("e", 3),
 )
 COUNTS = (("c", 1, 1, 0), ("x", 1, 2, 1), ("z", 1, 1, 0), ("z", 2, 4, 3))
 COUNT_MSGS = sum(up + down for _, _, up, down in COUNTS)

time: 63.3 us -> 61.6 us (0.973)
  Pallas kernels: 61 us -> 59.2 us
    pallas_call x1, Pallas kernels: 61 us -> 59.2 us  [on_device(): pl.pallas_call(functools.partial(kernel, nz, slots, tok), out_shape=jax.S...]
where the time goes in v6:
time: 61.6 us; the launch traced here: 61.4 us
  Pallas kernels  59.2 us (96%)
  local copies, waits for them, and re-layouts  1.55 us (3%)
  between operations  0.66 us (1%)
    pallas_call x1, Pallas kernels, on_device(): pl.pallas_call(functools.partial(kernel, nz, slots, tok), out_shape=jax.S...  59.2 us
    unnamed x1, local copies, waits for them, and re-layouts  1.55 us

profile of v6, /device:TPU:1, one launch (start us, length us, event | category | flops | bytes accessed | tf_op | source)
XLA Modules:
  0.0 61.4 jit_solution(3283761482855643086)
XLA Ops:
  0.7 59.2 %shard_map.73 = f32[16,1792]{1,0:T(8,128)} custom-call(bf16[192,1792]{1,0:T(8,128)(2,1)} %bitcast.3, bf16[192,1792]{1,0:T(8,128)(2,1)} %bitcast.4, bf16[192,512]{1,0:T(8,128)(2,1)} %bitcast.5, s32[1]{0:T(128)S(6)} %copy.9.arrival_hbm, s32[1,3]{1,0:T(1,128)} %owner_hbm.1, s32[1,3]{1,0:T(1,128)} %mult_hbm.1, s32[128]{0:T(128)} %pieces_hbm.1), custom_call_target="tpu_custom_call" | custom-call | tf_op jit(solution)/shard_map/pallas_call | solution.py:348
  59.9 1.6 %copy.10 = f32[16,1792]{1,0:T(8,128)} copy(f32[16,1792]{1,0:T(8,128)} %shard_map.73) | data formatting | bytes 229376

commit v7 on v6

--- a/solution.py
+++ b/solution.py
@@ -24,9 +24,9 @@
 )
 TREES = (TREE2, TREE2, TREE4, TREE4)
 ORDER = (
-    ("m", 0), ("z", 0, 0), ("f", 2), ("k", 0), ("m", 1), ("z", 1, 0), ("f", 3), ("z", 0, 1), ("k", 0),
-    ("m", 2), ("z", 2, 0), ("z", 1, 1), ("z", 0, 2), ("m", 3), ("z", 3, 0), ("z", 2, 1), ("z", 1, 2), ("z", 3, 1),
-    ("z", 2, 2), ("k", 0), ("z", 0, 3), ("z", 3, 2), ("z", 1, 3), ("e", 0), ("e", 1), ("e", 2), ("e", 3),
+    ("m", 0), ("z", 0, 0), ("f", 2), ("k", 0), ("m", 1), ("z", 1, 0), ("f", 3), ("z", 0, 1), ("m", 2),
+    ("z", 2, 0), ("m", 3), ("z", 3, 0), ("z", 1, 1), ("z", 2, 1), ("z", 0, 2), ("z", 3, 1), ("z", 1, 2), ("z", 2, 2),
+    ("k", 0), ("z", 3, 2), ("z", 0, 3), ("k", 0), ("z", 1, 3), ("e", 0), ("e", 1), ("e", 2), ("e", 3),
 )
 COUNTS = (("c", 1, 1, 0), ("x", 1, 2, 1), ("z", 1, 1, 0), ("z", 2, 4, 3))
 COUNT_MSGS = sum(up + down for _, _, up, down in COUNTS)

time: 61.6 us -> 61.2 us (level)
  Pallas kernels: 59.2 us -> 58.5 us
    pallas_call x1, Pallas kernels: 59.2 us -> 58.5 us  [on_device(): pl.pallas_call(functools.partial(kernel, nz, slots, tok), out_shape=jax.S...]
where the time goes in v7:
time: 61.2 us; the launch traced here: 60.7 us
  Pallas kernels  58.5 us (96%)
  local copies, waits for them, and re-layouts  1.55 us (3%)
  between operations  0.66 us (1%)
    pallas_call x1, Pallas kernels, on_device(): pl.pallas_call(functools.partial(kernel, nz, slots, tok), out_shape=jax.S...  58.5 us
    unnamed x1, local copies, waits for them, and re-layouts  1.55 us

profile of v7, /device:TPU:1, one launch (start us, length us, event | category | flops | bytes accessed | tf_op | source)
XLA Modules:
  0.0 60.7 jit_solution(8694622129147782022)
XLA Ops:
  0.7 58.5 %shard_map.73 = f32[16,1792]{1,0:T(8,128)} custom-call(bf16[192,1792]{1,0:T(8,128)(2,1)} %bitcast.3, bf16[192,1792]{1,0:T(8,128)(2,1)} %bitcast.4, bf16[192,512]{1,0:T(8,128)(2,1)} %bitcast.5, s32[1]{0:T(128)S(6)} %copy.9.arrival_hbm, s32[1,3]{1,0:T(1,128)} %owner_hbm.1, s32[1,3]{1,0:T(1,128)} %mult_hbm.1, s32[128]{0:T(128)} %pieces_hbm.1), custom_call_target="tpu_custom_call" | custom-call | tf_op jit(solution)/shard_map/pallas_call | solution.py:348
  59.1 1.6 %copy.10 = f32[16,1792]{1,0:T(8,128)} copy(f32[16,1792]{1,0:T(8,128)} %shard_map.73) | data formatting | bytes 229376

commit v8 on v7

--- a/solution.py
+++ b/solution.py
@@ -107,7 +107,6 @@
     barrier = pltpu.get_barrier_semaphore()
     for n in near:
         pl.semaphore_signal(barrier, inc=1, device_id=n, device_id_type=MESH)
-    pl.semaphore_wait(barrier, len(near))
 
     for d in loads[3:]:
         d.wait()
@@ -123,6 +122,7 @@
             here = (token + t * part >= k * tok) & (token + t * part < (k + 1) * tok)
             scale = jnp.where(here, weights[k].astype(jnp.float32), scale)
         W[t] = (cot[pl.ds(t * part, part), :].astype(jnp.float32) * scale).astype(jnp.bfloat16)
+    pl.semaphore_wait(barrier, len(near))
     for d in (2, 1, 3):
         send(W.at[(y + d) % NY], B.at[NY - d], dev(dy=d), s_b, r_b)
     B[0] = W[y]

time: 61.2 us -> 61.2 us (level)
  no operation moved by 1% of the time
where the time goes in v8:
time: 61.2 us; the launch traced here: 61.1 us
  Pallas kernels  58.9 us (96%)
  local copies, waits for them, and re-layouts  1.55 us (3%)
  between operations  0.66 us (1%)
    pallas_call x1, Pallas kernels, on_device(): pl.pallas_call(functools.partial(kernel, nz, slots, tok), out_shape=jax.S...  58.9 us
    unnamed x1, local copies, waits for them, and re-layouts  1.55 us

profile of v8, /device:TPU:1, one launch (start us, length us, event | category | flops | bytes accessed | tf_op | source)
XLA Modules:
  0.0 61.1 jit_solution(4264557671152304257)
XLA Ops:
  0.7 58.9 %shard_map.73 = f32[16,1792]{1,0:T(8,128)} custom-call(bf16[192,1792]{1,0:T(8,128)(2,1)} %bitcast.3, bf16[192,1792]{1,0:T(8,128)(2,1)} %bitcast.4, bf16[192,512]{1,0:T(8,128)(2,1)} %bitcast.5, s32[1]{0:T(128)S(6)} %copy.9.arrival_hbm, s32[1,3]{1,0:T(1,128)} %owner_hbm.1, s32[1,3]{1,0:T(1,128)} %mult_hbm.1, s32[128]{0:T(128)} %pieces_hbm.1), custom_call_target="tpu_custom_call" | custom-call | tf_op jit(solution)/shard_map/pallas_call | solution.py:348
  59.5 1.6 %copy.10 = f32[16,1792]{1,0:T(8,128)} copy(f32[16,1792]{1,0:T(8,128)} %shard_map.73) | data formatting | bytes 229376
